TPU v7x, 32 devices: a whole 2x2x4 slice. The times are simulated.
32 devices in a mesh: row: 8 (over z, y), col: 4 (over x, core).
Axes of the slice: x: 2, y: 2, z: 4, core: 2. Of those that a mesh axis runs over, the one named last changes fastest.
Arguments:
- density: bfloat16 [32, 12, 256, 256], P('row', 'col'), may hold values from -0.75 to 0.75
- col_list: int32 [32, 12], replicated, may hold values from 0 to 31, as said below
- orbital_position: bfloat16 [32, 3, 256], P('row'), may hold values from 0 to 1
- orbital_exponent: bfloat16 [32, 256], P('row'), may hold values from 0.019897461 to 3
- row_tiles: int32 [32, 6], P('row'), may hold values from 0 to 63, as said below
- tile_counts: int32 [8], replicated, may hold values from 0 to 16, as said below
- point_offset: bfloat16 [64, 3, 1024], replicated, may hold values from 0 to 1
- core_density: float32 [128, 1024], P('row', 'col'), may hold values from 0.025 to 8
- quad_weight: float32 [128, 1024], P('row', 'col'), may hold values from 0.2 to 2
Outputs:
- new_density: bfloat16 [32, 12, 256, 256], P('row', 'col')
- ks_blocks: float32 [32, 12, 256, 256], P('row', 'col')
- valence: float32 [128, 1024], P('row', 'col')
Inputs may be any that keep to these rules, and one draw needn't show every extreme that they name: `col_list`: entries g * 3 to g * 3 + 2 of block row a are 3 distinct block columns b with b modulo (4) equal to g, each within 8 of a cyclically modulo 32, in increasing order of the signed distance from a; a itself is listed. `row_tiles`: block row a lists 6 distinct tiles among 2 * a - 3 to 2 * a + 4 taken modulo 64, in increasing order of that offset. `tile_counts`: indices 2 * p and 2 * p + 1 of row together own the 16 tiles from 16 * p on; each index owns consecutive tiles, lower indices first; some index owns 16.
All inputs are finite; a program needn't handle non-finite values.
Results may differ from a plain program's by a relative error of at most 0.006.
Values may be sent and summed in bfloat16 or wider, within the bound.
A program may use at most 128 MiB of HBM per device.

v0:
```python
import math

import jax
import jax.numpy as jnp
from jax import lax
from jax.sharding import PartitionSpec as P

BAND = 8
REACH = 3


SLATER = 0.9847450218426965


def from_behind(value, axis, steps):
    count = lax.axis_size(axis)
    pairs = [(source, (source + steps) % count) for source in range(count)]
    return lax.ppermute(value, axis, pairs)


def basis_values(position, exponent, home_row, tile_id, tile_points, period):
    grid_x = tile_id.astype(jnp.float32) + tile_points[0]
    centre_x = 2.0 * home_row.astype(jnp.float32) + 2.0 * position[0]
    delta_x = jnp.mod(grid_x[None, :] - centre_x[:, None] + 0.5 * period, period) - 0.5 * period
    delta_y = tile_points[1][None, :] - position[1][:, None]
    delta_z = tile_points[2][None, :] - position[2][:, None]
    radius = delta_x * delta_x + delta_y * delta_y + delta_z * delta_z
    scaling = 1.0 / math.sqrt(position.shape[-1])
    return (jnp.exp(-exponent[:, None] * radius) * scaling).astype(jnp.bfloat16)


def potential(valence, core, weight):
    amount = core + jax.nn.softplus(valence)
    return weight * (-SLATER * jnp.cbrt(amount)) * jax.nn.sigmoid(valence)


def body(
    density,
    col_list,
    orbital_position,
    orbital_exponent,
    row_tiles,
    tile_counts,
    point_offset,
    core_density,
    quad_weight,
):
    highest = lax.Precision.HIGHEST
    rows_here = density.shape[0]
    group_size = density.shape[1]
    tiles_listed = row_tiles.shape[1]
    blocks_total = col_list.shape[0]
    period = 1.0 * point_offset.shape[0]
    row_count = lax.axis_size("row")
    row_index = lax.axis_index("row")
    col_index = lax.axis_index("col")
    reach_rows = -(-BAND // rows_here)
    base_row = (row_index - reach_rows) * rows_here
    pieces = []
    for offset in range(-reach_rows, reach_rows + 1):
        if offset == 0:
            pieces.append((density, orbital_position, orbital_exponent))
        else:
            pieces.append(
                from_behind((density, orbital_position, orbital_exponent), "row", -offset)
            )
    band_blocks = jnp.concatenate([member[0] for member in pieces], axis=0)
    band_position = jnp.concatenate([member[1] for member in pieces], axis=0)
    band_exponent = jnp.concatenate([member[2] for member in pieces], axis=0)
    full_row = lax.all_gather(density, "col", axis=1, tiled=True)
    new_rows = []
    partials = []
    tile_lists = []
    basis_store = []
    for local_row in range(rows_here):
        row_id = row_index * rows_here + local_row
        neighbours = jnp.take(col_list, row_id, axis=0)
        own_cols = lax.dynamic_slice_in_dim(neighbours, col_index * group_size, group_size)
        places = jnp.mod(neighbours - base_row, blocks_total)
        right_side = jnp.take(band_blocks, places, axis=0)
        right_cols = lax.dynamic_slice_in_dim(
            jnp.take(col_list, neighbours, axis=0), col_index * group_size, group_size, axis=1
        )
        matches = right_cols[None, :, :] == own_cols[:, None, None]
        chosen = jnp.zeros(
            (group_size,) + right_side.shape[:1] + right_side.shape[2:], jnp.bfloat16
        )
        for member in range(group_size):
            chosen = chosen + jnp.where(
                matches[:, :, member, None, None],
                right_side[None, :, member],
                jnp.zeros((), jnp.bfloat16),
            )
        square = jnp.einsum(
            "mxz,kmzy->kxy", full_row[local_row], chosen, preferred_element_type=jnp.float32
        )
        fresh = (2.0 * density[local_row].astype(jnp.float32) - square).astype(jnp.bfloat16)
        new_rows.append(fresh)
        tile_ids = row_tiles[local_row]
        tile_points = jnp.take(point_offset, tile_ids, axis=0).astype(jnp.float32)
        own_position = orbital_position[local_row].astype(jnp.float32)
        own_exponent = orbital_exponent[local_row].astype(jnp.float32)
        own_basis = jax.vmap(
            lambda tile_id, tile_spots: basis_values(
                own_position, own_exponent, row_id, tile_id, tile_spots, period
            )
        )(tile_ids, tile_points)
        column_places = jnp.mod(own_cols - base_row, blocks_total)
        column_position = jnp.take(band_position, column_places, axis=0).astype(jnp.float32)
        column_exponent = jnp.take(band_exponent, column_places, axis=0).astype(jnp.float32)

        def column_basis(position, exponent, column):
            return jax.vmap(
                lambda tile_id, tile_spots: basis_values(
                    position, exponent, column, tile_id, tile_spots, period
                )
            )(tile_ids, tile_points)

        other_basis = jax.vmap(column_basis)(column_position, column_exponent, own_cols)
        mixture = jnp.einsum(
            "kxy,ktyg->txg", fresh, other_basis, preferred_element_type=jnp.float32
        )
        partials.append(jnp.sum(own_basis.astype(jnp.float32) * mixture, axis=1))
        tile_lists.append(tile_ids)
        basis_store.append((own_basis, other_basis))
    partial_rows = jnp.concatenate(partials, axis=0)
    listed_tiles = jnp.concatenate(tile_lists, axis=0)
    shares = lax.psum_scatter(partial_rows, "col", scatter_dimension=1, tiled=True)
    slot_count = core_density.shape[0]
    upper_ends = jnp.cumsum(tile_counts)
    starts = upper_ends - tile_counts
    owners = jnp.sum((upper_ends[None, :] <= listed_tiles[:, None]).astype(jnp.int32), axis=1)
    slot_ids = listed_tiles - jnp.take(starts, owners)
    slot_range = jnp.arange(slot_count, dtype=jnp.int32)
    selectors = []
    valence = jnp.zeros((slot_count, shares.shape[1]), jnp.float32)
    for offset in range(-REACH, REACH + 1):
        target = jnp.mod(row_index + offset, row_count)
        selector = (
            (owners[None, :] == target) & (slot_ids[None, :] == slot_range[:, None])
        ).astype(jnp.float32)
        selectors.append(selector)
        packed = jnp.dot(selector, shares, precision=highest)
        if offset == 0:
            arrived = packed
        else:
            arrived = from_behind(packed, "row", offset)
        valence = valence + arrived
    field_vals = potential(valence, core_density, quad_weight)
    field_rows = jnp.zeros(shares.shape, jnp.float32)
    for position_index, offset in enumerate(range(-REACH, REACH + 1)):
        if offset == 0:
            arrived = field_vals
        else:
            arrived = from_behind(field_vals, "row", -offset)
        field_rows = field_rows + jnp.dot(selectors[position_index].T, arrived, precision=highest)
    field_full = lax.all_gather(field_rows, "col", axis=1, tiled=True)
    ks_rows = []
    for local_row in range(rows_here):
        own_basis, other_basis = basis_store[local_row]
        field_here = field_full[local_row * tiles_listed : (local_row + 1) * tiles_listed]
        weighted = (own_basis.astype(jnp.float32) * field_here[:, None, :]).astype(jnp.bfloat16)
        ks_rows.append(
            jnp.einsum("txg,ktyg->kxy", weighted, other_basis, preferred_element_type=jnp.float32)
        )
    return (jnp.stack(new_rows), jnp.stack(ks_rows), valence)


def solution(mesh):
    return jax.shard_map(
        body,
        mesh=mesh,
        in_specs=(
            P("row", "col", None, None),
            P(),
            P("row", None, None),
            P("row", None),
            P("row", None),
            P(),
            P(),
            P("row", "col"),
            P("row", "col"),
        ),
        out_specs=(P("row", "col", None, None), P("row", "col", None, None), P("row", "col")),
        check_vma=False,
    )
```

profile of v0, /device:TPU:0, one launch (start us, length us, event | category | flops | bytes accessed | tf_op | source)
XLA Modules:
  0.0 586.6 jit_solution(3781787855143198582)
XLA Ops:
  114.8 4.1 collective-permute-start.2
  128.2 56.6 %collective-permute-done.8 = bf16[4,3,256]{2,1,0:T(4,128)(2,1)S(1)} collective-permute-done((bf16[4,3,256]{2,1,0:T(4,128)(2,1)S(1)}, bf16[4,3,256]{2,1,0:T(4,128)(2,1)S(1)}, u32[]{:S(2)}, u32[]{:S(2)}) %collective-permute-start.8) | collective-permute-done | bytes 6176 | tf_op jit(solution)/shard_map/ppermute | solution.py:18
  186.1 5.1 collective-permute-done.9
  191.2 3.6 collective-permute-done.10
  195.2 3.6 collective-permute-done.11
  219.9 6.6 %gather_fusion.8 = bf16[12,3,256,256]{3,2,1,0:T(8,128)(2,1)} fusion(bf16[20,3,256,256]{3,2,1,0:T(8,128)(2,1)} %constant_dynamic-update-slice_fusion, s32[1024]{0:T(1024)} %pad_clamp_fusion.9), kind=kCustom, calls=%fused_computation.10.clone | custom fusion | bytes 9437232 | tf_op jit(solution)/shard_map/jit(_take)/gather | solution.py:80
  236.6 6.6 %gather_fusion.6 = bf16[12,3,256,256]{3,2,1,0:T(8,128)(2,1)} fusion(bf16[20,3,256,256]{3,2,1,0:T(8,128)(2,1)} %constant_dynamic-update-slice_fusion, s32[1024]{0:T(1024)} %pad_clamp_fusion.11), kind=kCustom, calls=%fused_computation.9.clone | custom fusion | bytes 9437232 | tf_op jit(solution)/shard_map/jit(_take)/gather | solution.py:80
  253.5 6.6 %gather_fusion.4 = bf16[12,3,256,256]{3,2,1,0:T(8,128)(2,1)} fusion(bf16[20,3,256,256]{3,2,1,0:T(8,128)(2,1)} %constant_dynamic-update-slice_fusion, s32[1024]{0:T(1024)} %pad_clamp_fusion.13), kind=kCustom, calls=%fused_computation.8.clone | custom fusion | bytes 9437232 | tf_op jit(solution)/shard_map/jit(_take)/gather | solution.py:80
  270.2 6.6 %gather_fusion.2 = bf16[12,3,256,256]{3,2,1,0:T(8,128)(2,1)} fusion(bf16[20,3,256,256]{3,2,1,0:T(8,128)(2,1)} %constant_dynamic-update-slice_fusion, s32[1024]{0:T(1024)} %pad_clamp_fusion.15), kind=kCustom, calls=%fused_computation.1.clone | custom fusion | bytes 9437232 | tf_op jit(solution)/shard_map/jit(_take)/gather | solution.py:80
  287.2 4.5 fusion.241
  291.9 36.6 %fusion.50 = f32[6,1024]{1,0:T(8,128)} fusion(f32[256]{0:T(256)S(1)} %bitcast.395, f32[6,1024]{1,0:T(8,128)S(1)} %copy-done.18, f32[256]{0:T(256)S(1)} %bitcast.397, f32[6,1024]{1,0:T(8,128)S(1)} %copy-done.20, f32[256]{0:T(256)S(1)} %bitcast.393, f32[6,1024]{1,0:T(8,128)S(1)} %copy-done.22, f32[256]{0:T(256)S(1)} %bitcast.373, f32[3,256]{1,0:T(4,128)S(1)} %bitcast.411, ...), kind=kOutput, calls=%fused_computation.91 | convolution fusion | flops 2540169216 | bytes 532480 | tf_op jit(solution)/shard_map/kxy,ktyg->txg/dot_general | solution.py:120
  330.4 25.9 %fusion.48 = f32[6,1024]{1,0:T(8,128)S(1)} fusion(f32[256]{0:T(256)S(1)} %bitcast.388, f32[6,1024]{1,0:T(8,128)S(1)} %copy-done.24, f32[256]{0:T(256)S(1)} %bitcast.386, f32[6,1024]{1,0:T(8,128)S(1)} %copy-done.26, f32[256]{0:T(256)S(1)} %bitcast.390, f32[6,1024]{1,0:T(8,128)S(1)} %copy-done.28, f32[256]{0:T(256)S(1)} %bitcast.370, ...), kind=kOutput, calls=%fused_computation.89 | convolution fusion | flops 2540169216 | bytes 532480 | tf_op jit(solution)/shard_map/kxy,ktyg->txg/dot_general | solution.py:120
  358.2 25.7 %fusion.46 = f32[6,1024]{1,0:T(8,128)S(1)} fusion(f32[256]{0:T(256)S(1)} %bitcast.382, f32[6,1024]{1,0:T(8,128)S(1)} %copy-done.36, f32[256]{0:T(256)S(1)} %bitcast.384, f32[6,1024]{1,0:T(8,128)S(1)} %copy-done.38, f32[256]{0:T(256)S(1)} %bitcast.380, f32[6,1024]{1,0:T(8,128)S(1)} %copy-done.40, f32[256]{0:T(256)S(1)} %bitcast.368, ...), kind=kOutput, calls=%fused_computation.87 | convolution fusion | flops 2540169216 | bytes 532480 | tf_op jit(solution)/shard_map/kxy,ktyg->txg/dot_general | solution.py:120
  385.8 26.1 %fusion.44 = f32[6,1024]{1,0:T(8,128)S(1)} fusion(f32[256]{0:T(256)S(1)} %bitcast.376, f32[6,1024]{1,0:T(8,128)S(1)} %copy-done.30, f32[256]{0:T(256)S(1)} %bitcast.374, f32[6,1024]{1,0:T(8,128)S(1)} %copy-done.32, f32[256]{0:T(256)S(1)} %bitcast.378, f32[6,1024]{1,0:T(8,128)S(1)} %copy-done.34, f32[256]{0:T(256)S(1)} %bitcast.366, ...), kind=kOutput, calls=%fused_computation.85 | convolution fusion | flops 2540169216 | bytes 532480 | tf_op jit(solution)/shard_map/kxy,ktyg->txg/dot_general | solution.py:120
  412.8 20.9 %reduce-scatter.2.cloned.1.call-done = f32[24,256]{1,0:T(8,128)} async-done(((f32[24,1024]{1,0:T(8,128)}), f32[24,256]{1,0:T(8,128)}) %reduce-scatter.2.cloned.1.call-update) | async-done | bytes 24592 | tf_op jit(solution)/shard_map/reduce_scatter | solution.py:128
  467.8 5.3 all_gather.7
  473.2 7.3 %fusion.410 = bf16[6,256,1024,1]{2,1,0,3:T(8,128)(2,1)S(1)} fusion(f32[6,1024]{1,0:T(8,128)S(1)} %get-tuple-element.82, f32[256]{0:T(256)} %bitcast.394, f32[6,1024]{1,0:T(8,128)S(1)} %copy-done.19, f32[256]{0:T(256)} %bitcast.396, f32[6,1024]{1,0:T(8,128)S(1)} %copy-done.21, f32[256]{0:T(256)} %bitcast.392, ...), kind=kLoop, calls=%fused_computation.189.clone.clone.clone.clone | loop fusion | flops 34603008 | bytes 3248128 | tf_op jit(solution)/shard_map/txg,ktyg->kxy/dot_general | solution.py:164
  480.7 19.4 %fusion.215 = f32[1,3,256,256]{2,3,1,0:T(8,128)S(1)} fusion(f32[6,1024]{1,0:T(8,128)S(1)} %copy-done.19, f32[6,1024]{1,0:T(8,128)S(1)} %copy-done.21, f32[3,256]{1,0:T(4,128)} %bitcast.410, f32[3,256]{1,0:T(4,128)} %bitcast.412, f32[3,256]{1,0:T(4,128)} %bitcast_add_fusion.4, f32[6,1024]{1,0:T(8,128)S(1)} %copy-done.45, f32[3,256]{1,0:T(4,128)} %convert_negate_fusion, ...), kind=kOutput, calls=%fused_computation.238 | convolution fusion | flops 2505572352 | bytes 4018176 | tf_op jit(solution)/shard_map/txg,ktyg->kxy/dot_general | solution.py:164
  500.2 6.7 %fusion.408 = bf16[6,256,1024,1]{2,1,0,3:T(8,128)(2,1)S(1)} fusion(f32[6,1024]{1,0:T(8,128)S(1)} %get-tuple-element.83, f32[256]{0:T(256)S(1)} %bitcast.389, f32[6,1024]{1,0:T(8,128)S(1)} %copy-done.25, f32[256]{0:T(256)S(1)} %bitcast.387, f32[6,1024]{1,0:T(8,128)S(1)} %copy-done.27, f32[256]{0:T(256)S(1)} %bitcast.391, ...), kind=kLoop, calls=%fused_computation.190.clone.clone.clone.clone | loop fusion | flops 34603008 | bytes 3248128 | tf_op jit(solution)/shard_map/txg,ktyg->kxy/dot_general | solution.py:164
  507.1 18.5 %fusion.210 = f32[1,3,256,256]{2,3,1,0:T(8,128)S(1)} fusion(f32[6,1024]{1,0:T(8,128)S(1)} %copy-done.25, f32[6,1024]{1,0:T(8,128)S(1)} %copy-done.27, f32[3,256]{1,0:T(4,128)S(1)} %bitcast.407, f32[3,256]{1,0:T(4,128)S(1)} %bitcast.409, f32[3,256]{1,0:T(4,128)S(1)} %copy-done.120, f32[6,1024]{1,0:T(8,128)S(1)} %copy-done.47, f32[3,256]{1,0:T(4,128)S(1)} %copy-done.113, ...), kind=kOutput, calls=%fused_computation.237 | convolution fusion | flops 2505572352 | bytes 4018176 | tf_op jit(solution)/shard_map/txg,ktyg->kxy/dot_general | solution.py:164
  525.7 7.0 %fusion.406 = bf16[6,256,1024,1]{2,1,0,3:T(8,128)(2,1)S(1)} fusion(f32[6,1024]{1,0:T(8,128)S(1)} %get-tuple-element.84, f32[256]{0:T(256)S(1)} %bitcast.383, f32[6,1024]{1,0:T(8,128)S(1)} %copy-done.37, f32[256]{0:T(256)S(1)} %bitcast.385, f32[6,1024]{1,0:T(8,128)S(1)} %copy-done.39, f32[256]{0:T(256)S(1)} %bitcast.381, ...), kind=kLoop, calls=%fused_computation.191.clone.clone.clone.clone | loop fusion | flops 34603008 | bytes 3248128 | tf_op jit(solution)/shard_map/txg,ktyg->kxy/dot_general | solution.py:164
  532.8 18.5 %fusion.205 = f32[1,3,256,256]{2,3,1,0:T(8,128)S(1)} fusion(f32[6,1024]{1,0:T(8,128)S(1)} %copy-done.37, f32[6,1024]{1,0:T(8,128)S(1)} %copy-done.39, f32[3,256]{1,0:T(4,128)S(1)} %bitcast.403, f32[3,256]{1,0:T(4,128)S(1)} %bitcast.405, f32[3,256]{1,0:T(4,128)S(1)} %copy-done.118, f32[6,1024]{1,0:T(8,128)S(1)} %copy-done.51, f32[3,256]{1,0:T(4,128)S(1)} %copy-done.111, ...), kind=kOutput, calls=%fused_computation.236 | convolution fusion | flops 2505572352 | bytes 4018176 | tf_op jit(solution)/shard_map/txg,ktyg->kxy/dot_general | solution.py:164
  551.4 6.8 %fusion.404 = bf16[6,256,1024,1]{2,1,0,3:T(8,128)(2,1)S(1)} fusion(f32[6,1024]{1,0:T(8,128)S(1)} %get-tuple-element.81, f32[256]{0:T(256)S(1)} %bitcast.377, f32[6,1024]{1,0:T(8,128)S(1)} %copy-done.31, f32[256]{0:T(256)S(1)} %bitcast.375, f32[6,1024]{1,0:T(8,128)S(1)} %copy-done.33, f32[256]{0:T(256)S(1)} %bitcast.379, ...), kind=kLoop, calls=%fused_computation.192.clone.clone.clone.clone.2 | loop fusion | flops 34603008 | bytes 3248128 | tf_op jit(solution)/shard_map/txg,ktyg->kxy/dot_general | solution.py:164
  558.3 18.6 %fusion.200 = f32[1,3,256,256]{2,3,1,0:T(8,128)S(1)} fusion(f32[6,1024]{1,0:T(8,128)S(1)} %copy-done.31, f32[6,1024]{1,0:T(8,128)S(1)} %copy-done.33, f32[3,256]{1,0:T(4,128)S(1)} %bitcast.399, f32[3,256]{1,0:T(4,128)S(1)} %bitcast.401, f32[3,256]{1,0:T(4,128)S(1)} %copy-done.116, f32[6,1024]{1,0:T(8,128)S(1)} %copy-done.49, f32[3,256]{1,0:T(4,128)S(1)} %copy-done.109, ...), kind=kOutput, calls=%fused_computation.235 | convolution fusion | flops 2505572352 | bytes 4018176 | tf_op jit(solution)/shard_map/txg,ktyg->kxy/dot_general | solution.py:164
  (516 shorter events, 222.8 us)
Async XLA Ops:
  7.2 279.9 %all-gather.2.cloned.1.call-start = ((), (), s32[]{:S(2)}) async-start(), calls=%async_computation.1 | async-start | bytes 7864320 | tf_op jit(solution)/shard_map/all_gather | solution.py:70
  7.9 425.7 %reduce-scatter.2.cloned.1.call-start = ((), (), s32[]{:S(2)}) async-start(), calls=%async_computation.2 | async-start | bytes 122880 | tf_op jit(solution)/shard_map/reduce_scatter | solution.py:128
  8.0 201.3 %collective-permute-start = (bf16[4,3,256,256]{3,2,1,0:T(8,128)(2,1)}, bf16[4,3,256,256]{3,2,1,0:T(8,128)(2,1)S(1)}, u32[]{:S(2)}, u32[]{:S(2)}) collective-permute-start(bf16[4,3,256,256]{3,2,1,0:T(8,128)(2,1)} %param.21), channel_id=1, source_target_pairs={{0,8},{4,12},{8,16},{12,20},{16,24},{20,28},{24,0},{28,4},{1,9},{5... | collective-permute-start | bytes 4718600 | tf_op jit(solution)/shard_map/ppermute | solution.py:18
  11.1 103.1 %collective-permute-start.4 = (bf16[4,256]{1,0:T(4,128)(2,1)}, bf16[4,256]{1,0:T(4,128)(2,1)}, u32[]{:S(2)}, u32[]{:S(2)}) collective-permute-start(bf16[4,256]{1,0:T(4,128)(2,1)} %param.24), channel_id=1, source_target_pairs={{0,8},{4,12},{8,16},{12,20},{16,24},{20,28},{24,0},{28,4},{1,9},{5... | collective-permute-start | bytes 6152 | tf_op jit(solution)/shard_map/ppermute | solution.py:18
  12.7 102.2 %collective-permute-start.5 = (bf16[4,256]{1,0:T(4,128)(2,1)}, bf16[4,256]{1,0:T(4,128)(2,1)}, u32[]{:S(2)}, u32[]{:S(2)}) collective-permute-start(bf16[4,256]{1,0:T(4,128)(2,1)} %param.24), channel_id=1, source_target_pairs={{0,4},{4,8},{8,12},{12,16},{16,20},{20,24},{24,28},{28,0},{1,5},{5... | collective-permute-start | bytes 6152 | tf_op jit(solution)/shard_map/ppermute | solution.py:18
  14.2 104.7 %collective-permute-start.6 = (bf16[4,256]{1,0:T(4,128)(2,1)}, bf16[4,256]{1,0:T(4,128)(2,1)}, u32[]{:S(2)}, u32[]{:S(2)}) collective-permute-start(bf16[4,256]{1,0:T(4,128)(2,1)} %param.24), channel_id=1, source_target_pairs={{0,28},{4,0},{8,4},{12,8},{16,12},{20,16},{24,20},{28,24},{1,29},{... | collective-permute-start | bytes 6152 | tf_op jit(solution)/shard_map/ppermute | solution.py:18
  17.4 101.5 %collective-permute-start.7 = (bf16[4,256]{1,0:T(4,128)(2,1)}, bf16[4,256]{1,0:T(4,128)(2,1)}, u32[]{:S(2)}, u32[]{:S(2)}) collective-permute-start(bf16[4,256]{1,0:T(4,128)(2,1)} %param.24), channel_id=1, source_target_pairs={{0,24},{4,28},{8,0},{12,4},{16,8},{20,12},{24,16},{28,20},{1,25},{... | collective-permute-start | bytes 6152 | tf_op jit(solution)/shard_map/ppermute | solution.py:18
  114.2 96.4 %collective-permute-start.1 = (bf16[4,3,256,256]{3,2,1,0:T(8,128)(2,1)S(1)}, bf16[4,3,256,256]{3,2,1,0:T(8,128)(2,1)}, u32[]{:S(2)}, u32[]{:S(2)}) collective-permute-start(bf16[4,3,256,256]{3,2,1,0:T(8,128)(2,1)S(1)} %copy-done.2), channel_id=1, source_target_pairs={{0,4},{4,8},{8,12},{12,16},{16,20},{20,24},{24,28},{28,0},{1,5},{5... | collective-permute-start | bytes 4718600 | tf_op jit(solution)/shard_map/ppermute | solution.py:18
  114.8 99.6 %collective-permute-start.2 = (bf16[4,3,256,256]{3,2,1,0:T(8,128)(2,1)S(1)}, bf16[4,3,256,256]{3,2,1,0:T(8,128)(2,1)}, u32[]{:S(2)}, u32[]{:S(2)}) collective-permute-start(bf16[4,3,256,256]{3,2,1,0:T(8,128)(2,1)S(1)} %copy-done.2), channel_id=1, source_target_pairs={{0,28},{4,0},{8,4},{12,8},{16,12},{20,16},{24,20},{28,24},{1,29},{... | collective-permute-start | bytes 4718600 | tf_op jit(solution)/shard_map/ppermute | solution.py:18
  118.9 98.3 %collective-permute-start.3 = (bf16[4,3,256,256]{3,2,1,0:T(8,128)(2,1)S(1)}, bf16[4,3,256,256]{3,2,1,0:T(8,128)(2,1)}, u32[]{:S(2)}, u32[]{:S(2)}) collective-permute-start(bf16[4,3,256,256]{3,2,1,0:T(8,128)(2,1)S(1)} %copy-done.2), channel_id=1, source_target_pairs={{0,24},{4,28},{8,0},{12,4},{16,8},{20,12},{24,16},{28,20},{1,25},{... | collective-permute-start | bytes 4718600 | tf_op jit(solution)/shard_map/ppermute | solution.py:18
  118.9 65.9 %collective-permute-start.8 = (bf16[4,3,256]{2,1,0:T(4,128)(2,1)S(1)}, bf16[4,3,256]{2,1,0:T(4,128)(2,1)S(1)}, u32[]{:S(2)}, u32[]{:S(2)}) collective-permute-start(bf16[4,3,256]{2,1,0:T(4,128)(2,1)S(1)} %copy.109), channel_id=1, source_target_pairs={{0,8},{4,12},{8,16},{12,20},{16,24},{20,28},{24,0},{28,4},{1,9},{5... | collective-permute-start | bytes 18440 | tf_op jit(solution)/shard_map/ppermute | solution.py:18
  184.9 6.3 %collective-permute-start.9 = (bf16[4,3,256]{2,1,0:T(4,128)(2,1)S(1)}, bf16[4,3,256]{2,1,0:T(4,128)(2,1)S(1)}, u32[]{:S(2)}, u32[]{:S(2)}) collective-permute-start(bf16[4,3,256]{2,1,0:T(4,128)(2,1)S(1)} %copy.109), channel_id=1, source_target_pairs={{0,4},{4,8},{8,12},{12,16},{16,20},{20,24},{24,28},{28,0},{1,5},{5... | collective-permute-start | bytes 18440 | tf_op jit(solution)/shard_map/ppermute | solution.py:18
  194.9 4.0 collective-permute-start.11
  434.6 13.0 %collective-permute-start.17 = (f32[16,256]{1,0:T(8,128)S(1)}, f32[16,256]{1,0:T(8,128)S(1)}, u32[]{:S(2)}, u32[]{:S(2)}) collective-permute-start(f32[16,256]{1,0:T(8,128)S(1)} %fusion.290), channel_id=1, source_target_pairs={{0,12},{4,16},{8,20},{12,24},{16,28},{20,0},{24,4},{28,8},{1,13},{... | collective-permute-start | bytes 49160 | tf_op jit(solution)/shard_map/ppermute | solution.py:18
  437.9 12.1 %collective-permute-start.16 = (f32[16,256]{1,0:T(8,128)S(1)}, f32[16,256]{1,0:T(8,128)S(1)}, u32[]{:S(2)}, u32[]{:S(2)}) collective-permute-start(f32[16,256]{1,0:T(8,128)S(1)} %fusion.286), channel_id=1, source_target_pairs={{0,8},{4,12},{8,16},{12,20},{16,24},{20,28},{24,0},{28,4},{1,9},{5... | collective-permute-start | bytes 49160 | tf_op jit(solution)/shard_map/ppermute | solution.py:18
  440.3 9.8 %collective-permute-start.15 = (f32[16,256]{1,0:T(8,128)S(1)}, f32[16,256]{1,0:T(8,128)S(1)}, u32[]{:S(2)}, u32[]{:S(2)}) collective-permute-start(f32[16,256]{1,0:T(8,128)S(1)} %fusion.282), channel_id=1, source_target_pairs={{0,4},{4,8},{8,12},{12,16},{16,20},{20,24},{24,28},{28,0},{1,5},{5... | collective-permute-start | bytes 49160 | tf_op jit(solution)/shard_map/ppermute | solution.py:18
  442.6 7.4 %collective-permute-start.14 = (f32[16,256]{1,0:T(8,128)S(1)}, f32[16,256]{1,0:T(8,128)S(1)}, u32[]{:S(2)}, u32[]{:S(2)}) collective-permute-start(f32[16,256]{1,0:T(8,128)S(1)} %fusion.273), channel_id=1, source_target_pairs={{0,28},{4,0},{8,4},{12,8},{16,12},{20,16},{24,20},{28,24},{1,29},{... | collective-permute-start | bytes 49160 | tf_op jit(solution)/shard_map/ppermute | solution.py:18
  446.7 4.6 collective-permute-start.12
  447.6 3.8 collective-permute-start.13
  452.2 12.7 %collective-permute-start.23 = (f32[16,256]{1,0:T(8,128)S(1)}, f32[16,256]{1,0:T(8,128)S(1)}, u32[]{:S(2)}, u32[]{:S(2)}) collective-permute-start(f32[16,256]{1,0:T(8,128)S(1)} %get-tuple-element.166), channel_id=1, source_target_pairs={{0,20},{4,24},{8,28},{12,0},{16,4},{20,8},{24,12},{28,16},{1,21},{... | collective-permute-start | bytes 49160 | tf_op jit(solution)/shard_map/ppermute | solution.py:18
  454.6 10.5 %collective-permute-start.22 = (f32[16,256]{1,0:T(8,128)S(1)}, f32[16,256]{1,0:T(8,128)S(1)}, u32[]{:S(2)}, u32[]{:S(2)}) collective-permute-start(f32[16,256]{1,0:T(8,128)S(1)} %get-tuple-element.166), channel_id=1, source_target_pairs={{0,24},{4,28},{8,0},{12,4},{16,8},{20,12},{24,16},{28,20},{1,25},{... | collective-permute-start | bytes 49160 | tf_op jit(solution)/shard_map/ppermute | solution.py:18
  457.4 6.4 %collective-permute-start.20 = (f32[16,256]{1,0:T(8,128)S(1)}, f32[16,256]{1,0:T(8,128)S(1)}, u32[]{:S(2)}, u32[]{:S(2)}) collective-permute-start(f32[16,256]{1,0:T(8,128)S(1)} %get-tuple-element.166), channel_id=1, source_target_pairs={{0,4},{4,8},{8,12},{12,16},{16,20},{20,24},{24,28},{28,0},{1,5},{5... | collective-permute-start | bytes 49160 | tf_op jit(solution)/shard_map/ppermute | solution.py:18
  457.7 6.4 %collective-permute-start.19 = (f32[16,256]{1,0:T(8,128)S(1)}, f32[16,256]{1,0:T(8,128)S(1)}, u32[]{:S(2)}, u32[]{:S(2)}) collective-permute-start(f32[16,256]{1,0:T(8,128)S(1)} %get-tuple-element.166), channel_id=1, source_target_pairs={{0,8},{4,12},{8,16},{12,20},{16,24},{20,28},{24,0},{28,4},{1,9},{5... | collective-permute-start | bytes 49160 | tf_op jit(solution)/shard_map/ppermute | solution.py:18
  458.3 6.4 %collective-permute-start.18 = (f32[16,256]{1,0:T(8,128)S(1)}, f32[16,256]{1,0:T(8,128)S(1)}, u32[]{:S(2)}, u32[]{:S(2)}) collective-permute-start(f32[16,256]{1,0:T(8,128)S(1)} %get-tuple-element.166), channel_id=1, source_target_pairs={{0,12},{4,16},{8,20},{12,24},{16,28},{20,0},{24,4},{28,8},{1,13},{... | collective-permute-start | bytes 49160 | tf_op jit(solution)/shard_map/ppermute | solution.py:18
  (151 other events, 3438.9 us)
Sparse Core Ops, SparseCore 0:
  9.6 49.0 all-gather.1
  412.8 20.7 reduce-scatter.1
where the time goes:
time: 588 us; the launch traced here: 587 us
  matrix products  206 us (35%)
  local copies, waits for them, and re-layouts  114 us (19%)
  other arithmetic  111 us (19%)
  waiting for transfers between devices  98.1 us (17%)
  starting transfers between devices  35.6 us (6%)
  between operations  16.7 us (3%)
    dot_general x4, matrix products, body(): jnp.einsum('kxy,ktyg->txg', fresh, other_basis, preferred_element_type=jn...  114 us
    ppermute x24, waiting for transfers between devices, from_behind(): return lax.ppermute(value, axis, pairs)  76.5 us
    dot_general x4, matrix products, body(): jnp.einsum('txg,ktyg->kxy', weighted, other_basis, preferred_element_type...  75.1 us
    ppermute x24, starting transfers between devices, from_behind(): return lax.ppermute(value, axis, pairs)  35.5 us
    broadcast_in_dim x20, local copies, waits for them, and re-layouts, body(): jnp.where(matches[:, :, member, None, None], right_side[None, :, member],...  31.9 us
    unnamed x322, local copies, waits for them, and re-layouts  28.2 us
    dot_general x4, other arithmetic, body(): jnp.einsum('txg,ktyg->kxy', weighted, other_basis, preferred_element_type...  27.9 us
    gather x4, local copies, waits for them, and re-layouts, body(): right_side = jnp.take(band_blocks, places, axis=0)  26.2 us
  transfers between devices with their start and end apart: 26, of which 9 were waited for; matrix products, arithmetic and copies ran while one was open for 34% of the time, Pallas kernels for 0%

commit v1 on v0

v1 whole, which is shorter than its diff:
```python
import functools
import math

import jax
import jax.numpy as jnp
from jax import lax
from jax.experimental import pallas as pl
from jax.experimental.pallas import tpu as pltpu
from jax.sharding import PartitionSpec as P

BAND = 8
REACH = 3
SLATER = 0.9847450218426965
LOG2E = 1.4426950408889634


def from_behind(value, axis, steps):
    count = lax.axis_size(axis)
    pairs = [(source, (source + steps) % count) for source in range(count)]
    return lax.ppermute(value, axis, pairs)


def potential(valence, core, weight):
    amount = core + jax.nn.softplus(valence)
    return weight * (-SLATER * jnp.cbrt(amount)) * jax.nn.sigmoid(valence)


def split3(x):
    high = x.astype(jnp.bfloat16).astype(jnp.float32)
    rest = x - high
    mid = rest.astype(jnp.bfloat16).astype(jnp.float32)
    return high, mid, rest - mid


def point_features(pts):
    pts = pts.astype(jnp.float32)
    ox, oy, oz = pts[0:1], pts[1:2], pts[2:3]
    square = ox * ox + oy * oy + oz * oz
    row = lax.broadcasted_iota(jnp.int32, (8, pts.shape[1]), 0)
    feats = jnp.where(row == 0, square, 0.0)
    feats = jnp.where(row == 1, ox, feats)
    feats = jnp.where(row == 2, oy, feats)
    feats = jnp.where(row == 3, oz, feats)
    feats = jnp.where(row == 4, 1.0, feats)
    high, mid, low = split3(feats)
    return jnp.concatenate([high, high, high, mid, mid, low], axis=0).astype(jnp.bfloat16)


def orbital_features(params, shift):
    size = params.shape[1]
    px, py, pz = params[0:1], params[1:2], params[2:3]
    scaled = params[3:4] * LOG2E
    px = 2.0 * px - shift
    row = lax.broadcasted_iota(jnp.int32, (8, size), 0)
    const = -scaled * (px * px + py * py + pz * pz) - 0.5 * math.log2(size)
    feats = jnp.where(row == 0, -scaled, 0.0)
    feats = jnp.where(row == 1, 2.0 * scaled * px, feats)
    feats = jnp.where(row == 2, 2.0 * scaled * py, feats)
    feats = jnp.where(row == 3, 2.0 * scaled * pz, feats)
    feats = jnp.where(row == 4, const, feats)
    high, mid, low = split3(feats)
    return jnp.concatenate([high, mid, low, high, mid, high], axis=0).astype(jnp.bfloat16)


def fill_basis(phi_ref, par_ref, pts_ref, tiles_ref, shift_ref, row, j):
    members, size = par_ref.shape[1], par_ref.shape[3]
    feats = point_features(pts_ref[tiles_ref[row, j]])
    for member in range(members):
        shift = shift_ref[row, j * members + member].astype(jnp.float32)
        coefs = orbital_features(par_ref[0, member], shift)
        expo = lax.dot_general(
            coefs, feats, (((0,), (0,)), ((), ())), preferred_element_type=jnp.float32
        )
        phi_ref[member * size : (member + 1) * size, :] = jnp.exp2(expo).astype(jnp.bfloat16)


def square_kernel(
    pick_ref, tiles_ref, shift_ref, full_ref, par_ref, pts_ref, *rest
):
    pieces = rest[:-6]
    new_ref, part_ref, band, newcat, phi, sem = rest[-6:]
    row = pl.program_id(0)
    groups, kg, size = full_ref.shape[0], full_ref.shape[2], full_ref.shape[3]
    per_piece = pieces[0].shape[0]

    @pl.when(row == 0)
    def _():
        copies = [
            pltpu.make_async_copy(piece, band.at[pl.ds(at * per_piece, per_piece)], sem.at[at])
            for at, piece in enumerate(pieces)
        ]
        for copy in copies:
            copy.start()
        band[len(pieces) * per_piece] = jnp.zeros((size, size), jnp.bfloat16)
        for copy in copies:
            copy.wait()

    own_at = (len(pieces) // 2) * per_piece + row * kg
    for k in range(kg):
        acc = jnp.zeros((size, size), jnp.float32)
        for m in range(groups * kg):
            acc = acc + jnp.dot(
                full_ref[m // kg, 0, m % kg],
                band[pick_ref[row, k * groups * kg + m]],
                preferred_element_type=jnp.float32,
            )
        fresh = (2.0 * band[own_at + k].astype(jnp.float32) - acc).astype(jnp.bfloat16)
        new_ref[0, k] = fresh
        newcat[:, k * size : (k + 1) * size] = fresh

    points = phi.shape[1]

    def step(j, carry):
        fill_basis(phi, par_ref, pts_ref, tiles_ref, shift_ref, row, j)
        for at in range(points // size):
            cols = slice(at * size, (at + 1) * size)
            mix = jnp.dot(newcat[...], phi[size:, cols], preferred_element_type=jnp.float32)
            own = phi[:size, cols].astype(jnp.float32)
            part_ref[0, pl.ds(j, 1), cols] = jnp.sum(own * mix, axis=0, keepdims=True)
        return carry

    lax.fori_loop(0, tiles_ref.shape[1], step, 0)


def ks_kernel(tiles_ref, shift_ref, holder_ref, par_ref, pts_ref, field_ref, out_ref, phi):
    row = pl.program_id(0)
    kg, size = out_ref.shape[1], out_ref.shape[2]
    out_ref[...] = jnp.zeros(out_ref.shape, jnp.float32)

    def step(j, carry):
        fill_basis(phi, par_ref, pts_ref, tiles_ref, shift_ref, row, j)
        field = field_ref[pl.ds(holder_ref[row, j], 1), :]
        weighted = (phi[:size].astype(jnp.float32) * field).astype(jnp.bfloat16)
        for k in range(kg):
            out_ref[0, k] += lax.dot_general(
                weighted,
                phi[(k + 1) * size : (k + 2) * size],
                (((1,), (1,)), ((), ())),
                preferred_element_type=jnp.float32,
            )
        return carry

    lax.fori_loop(0, tiles_ref.shape[1], step, 0)


def body(
    density,
    col_list,
    orbital_position,
    orbital_exponent,
    row_tiles,
    tile_counts,
    point_offset,
    core_density,
    quad_weight,
):
    highest = lax.Precision.HIGHEST
    rows_here, kg, size = density.shape[:3]
    tiles_listed = row_tiles.shape[1]
    blocks_total, neighbours_listed = col_list.shape
    tiles_total, _, points = point_offset.shape
    row_count = lax.axis_size("row")
    groups = lax.axis_size("col")
    row_index = lax.axis_index("row")
    col_index = lax.axis_index("col")
    reach_rows = -(-BAND // rows_here)
    base_row = (row_index - reach_rows) * rows_here
    flat = density.reshape(rows_here * kg, size, size)
    pieces = [
        flat if offset == 0 else from_behind(flat, "row", -offset)
        for offset in range(-reach_rows, reach_rows + 1)
    ]
    full = lax.all_gather(density, "col", axis=0)
    orbitals = jnp.concatenate([orbital_position, orbital_exponent[:, None]], axis=1)
    orbitals = lax.all_gather(orbitals, "row", axis=0, tiled=True)

    row_ids = row_index * rows_here + jnp.arange(rows_here, dtype=jnp.int32)
    lists = lax.dynamic_slice_in_dim(col_list, row_index * rows_here, rows_here, axis=0)
    own_cols = lax.dynamic_slice_in_dim(lists, col_index * kg, kg, axis=1)
    places = jnp.mod(lists - base_row, blocks_total)
    group_lists = lax.dynamic_slice_in_dim(col_list, col_index * kg, kg, axis=1)
    right_cols = jnp.take(group_lists, lists, axis=0)
    matches = right_cols[:, None, :, :] == own_cols[:, :, None, None]
    zero_block = len(pieces) * rows_here * kg
    flat_at = places[:, None, :, None] * kg + jnp.arange(kg, dtype=jnp.int32)
    pick = jnp.min(jnp.where(matches, flat_at, zero_block), axis=-1)
    pick = pick.reshape(rows_here, kg * neighbours_listed)

    members = jnp.concatenate([row_ids[:, None], own_cols], axis=1)
    params = jnp.take(orbitals, members, axis=0).astype(jnp.float32)
    params = jnp.pad(params, ((0, 0), (0, 0), (0, 4), (0, 0)))
    half = tiles_total // 2
    shift = row_tiles[:, :, None] - 2 * members[:, None, :]
    shift = jnp.mod(shift + half, tiles_total) - half
    shift = shift.reshape(rows_here, tiles_listed * (kg + 1))

    whole = lambda shape: pl.BlockSpec(shape, lambda i, *_: (0,) * len(shape))
    par_spec = pl.BlockSpec((1, kg + 1, 8, size), lambda i, *_: (i, 0, 0, 0))
    basis_flops = 2 * rows_here * tiles_listed * (kg + 1) * size * points * size
    new_density, partial = pl.pallas_call(
        square_kernel,
        out_shape=(
            jax.ShapeDtypeStruct(density.shape, jnp.bfloat16),
            jax.ShapeDtypeStruct((rows_here, tiles_listed, points), jnp.float32),
        ),
        grid_spec=pltpu.PrefetchScalarGridSpec(
            num_scalar_prefetch=3,
            grid=(rows_here,),
            in_specs=[
                pl.BlockSpec((groups, 1, kg, size, size), lambda i, *_: (0, i, 0, 0, 0)),
                par_spec,
                whole(point_offset.shape),
            ]
            + [pl.BlockSpec(memory_space=pl.ANY)] * len(pieces),
            out_specs=(
                pl.BlockSpec((1, kg, size, size), lambda i, *_: (i, 0, 0, 0)),
                pl.BlockSpec((1, tiles_listed, points), lambda i, *_: (i, 0, 0)),
            ),
            scratch_shapes=[
                pltpu.VMEM((zero_block + 1, size, size), jnp.bfloat16),
                pltpu.VMEM((size, kg * size), jnp.bfloat16),
                pltpu.VMEM(((kg + 1) * size, points), jnp.bfloat16),
                pltpu.SemaphoreType.DMA((len(pieces),)),
            ],
        ),
        compiler_params=pltpu.CompilerParams(dimension_semantics=("arbitrary",)),
        cost_estimate=pl.CostEstimate(
            flops=2 * basis_flops, bytes_accessed=20_000_000, transcendentals=0
        ),
        name="square_collocate",
    )(pick, row_tiles, shift, full, params, point_offset, *pieces)

    shares = lax.psum_scatter(
        partial.reshape(rows_here * tiles_listed, points), "col", scatter_dimension=1, tiled=True
    )
    reach_tiles = 2 * REACH
    window = -(-(2 * rows_here + reach_tiles) // 8) * 8
    first = 2 * rows_here * row_index - REACH
    spot = jnp.mod(row_tiles.reshape(-1) - first, tiles_total)
    spots = jnp.arange(window, dtype=jnp.int32)
    packed = jnp.dot(
        (spots[:, None] == spot[None, :]).astype(jnp.float32), shares, precision=highest
    )
    gathered = lax.all_gather(packed, "row", axis=0, tiled=True)
    upper_ends = jnp.cumsum(tile_counts)
    starts = upper_ends - tile_counts
    slot_count = core_density.shape[0]
    slots = jnp.arange(slot_count, dtype=jnp.int32)
    my_start = jnp.take(starts, row_index)
    my_tiles = jnp.where(slots < jnp.take(tile_counts, row_index), my_start + slots, -1)
    senders = jnp.arange(row_count, dtype=jnp.int32)
    sent_tiles = jnp.mod(
        (2 * rows_here * senders - REACH)[:, None] + spots[None, :], tiles_total
    ).reshape(-1)
    valence = jnp.dot(
        (my_tiles[:, None] == sent_tiles[None, :]).astype(jnp.float32), gathered, precision=highest
    )
    field = potential(valence, core_density, quad_weight)
    field = lax.all_gather(field, "row", axis=0, tiled=True)
    field = lax.all_gather(field, "col", axis=1, tiled=True)
    owners = jnp.sum((upper_ends <= row_tiles[:, :, None]).astype(jnp.int32), axis=-1)
    holder = owners * slot_count + row_tiles - jnp.take(starts, owners)

    ks = pl.pallas_call(
        ks_kernel,
        out_shape=jax.ShapeDtypeStruct(density.shape, jnp.float32),
        grid_spec=pltpu.PrefetchScalarGridSpec(
            num_scalar_prefetch=3,
            grid=(rows_here,),
            in_specs=[par_spec, whole(point_offset.shape), whole(field.shape)],
            out_specs=pl.BlockSpec((1, kg, size, size), lambda i, *_: (i, 0, 0, 0)),
            scratch_shapes=[pltpu.VMEM(((kg + 1) * size, points), jnp.bfloat16)],
        ),
        compiler_params=pltpu.CompilerParams(dimension_semantics=("arbitrary",)),
        cost_estimate=pl.CostEstimate(
            flops=2 * basis_flops, bytes_accessed=5_000_000, transcendentals=0
        ),
        name="ks_blocks",
    )(row_tiles, shift, holder, params, point_offset, field)
    return (new_density, ks, valence)


def solution(mesh):
    return jax.shard_map(
        body,
        mesh=mesh,
        in_specs=(
            P("row", "col", None, None),
            P(),
            P("row", None, None),
            P("row", None),
            P("row", None),
            P(),
            P(),
            P("row", "col"),
            P("row", "col"),
        ),
        out_specs=(P("row", "col", None, None), P("row", "col", None, None), P("row", "col")),
        check_vma=False,
    )
```

time: 588 us -> 310 us (0.53)
  matrix products: 206 us -> 1.68 us
  blocking collectives: 5.33 us -> 183 us
  other arithmetic: 111 us -> 2.81 us
  local copies, waits for them, and re-layouts: 114 us -> 8.71 us
  waiting for transfers between devices: 98.1 us -> 18.7 us
  Pallas kernels: 0 us -> 71.6 us
  starting transfers between devices: 35.6 us -> 8.14 us
    dot_general x26 -> x2, matrix products: 206 us -> 1.68 us  [the longest x1 0.86 us: body(): jnp.dot((spots[:, None] == spot[None, :]).astype(jnp.float32), shares, pr...]
    all_gather x1 -> x4, blocking collectives: 5.33 us -> 183 us  [the longest x1 115 us: body(): orbitals = lax.all_gather(orbitals, 'row', axis=0, tiled=True)]
    ppermute x24 -> x4, waiting for transfers between devices: 76.5 us -> 0.01 us  [from_behind(): return lax.ppermute(value, axis, pairs)]
    pallas_call x0 -> x2, Pallas kernels: none -> 71.6 us  [the longest x1 40.4 us: body(): pl.pallas_call(square_kernel, out_shape=(jax.ShapeDtypeStruct(density.sha...]
    gather x21 -> x6, local copies, waits for them, and re-layouts: 43.7 us -> 2.12 us  [the longest x2 0.78 us: body(): holder = owners * slot_count + row_tiles - jnp.take(starts, owners)]
    broadcast_in_dim x20 -> x2, local copies, waits for them, and re-layouts: 31.9 us -> 0.09 us  [the longest x1 0.08 us: body(): right_cols = jnp.take(group_lists, lists, axis=0)]
    dot_general x4 -> x0, other arithmetic: 27.9 us -> none  [body(): jnp.einsum('txg,ktyg->kxy', weighted, other_basis, preferred_element_type...]
    ppermute x24 -> x4, starting transfers between devices: 35.5 us -> 8.06 us  [from_behind(): return lax.ppermute(value, axis, pairs)]
  transfers between devices with their start and end apart: 26 -> 6, of which waited for: 9 -> 1; matrix products, arithmetic and copies ran while one was open for 34% -> 3% of each run, Pallas kernels for 0% -> 0%
where the time goes in v1:
time: 310 us
  blocking collectives  183 us (59%)
  Pallas kernels  71.6 us (23%)
  waiting for transfers between devices  18.7 us (6%)
  between operations  15.5 us (5%)
  local copies, waits for them, and re-layouts  8.71 us (3%)
  starting transfers between devices  8.14 us (3%)
    all_gather x1, blocking collectives, body(): orbitals = lax.all_gather(orbitals, 'row', axis=0, tiled=True)  115 us
    pallas_call x1, Pallas kernels, body(): pl.pallas_call(square_kernel, out_shape=(jax.ShapeDtypeStruct(density.sha...  40.4 us
    pallas_call x1, Pallas kernels, body(): pl.pallas_call(ks_kernel, out_shape=jax.ShapeDtypeStruct(density.shape, j...  31.2 us
    all_gather x1, blocking collectives, body(): gathered = lax.all_gather(packed, 'row', axis=0, tiled=True)  30.6 us
    all_gather x1, blocking collectives, body(): field = lax.all_gather(field, 'row', axis=0, tiled=True)  30.5 us
    reduce_scatter x1, waiting for transfers between devices, body(): lax.psum_scatter(partial.reshape(rows_here * tiles_listed, points), 'col'...  18 us
    ppermute x4, starting transfers between devices, from_behind(): return lax.ppermute(value, axis, pairs)  8.06 us
    all_gather x1, blocking collectives, body(): field = lax.all_gather(field, 'col', axis=1, tiled=True)  6.94 us
  transfers between devices with their start and end apart: 6, of which 1 were waited for; matrix products, arithmetic and copies ran while one was open for 3% of the time, Pallas kernels for 0%

profile of v1, /device:TPU:0, one launch (start us, length us, event | category | flops | bytes accessed | tf_op | source)
XLA Modules:
  0.0 309.9 jit_solution(8816653623349684650)
XLA Ops:
  7.3 0.7 all-gather.3.cloned.1.call-update
  8.6 3.1 collective-permute-start
  11.6 1.5 collective-permute-start.1
  13.2 3.2 %collective-permute-start.2 = (bf16[12,256,256]{2,1,0:T(8,128)(2,1)S(1)}, bf16[12,256,256]{2,1,0:T(8,128)(2,1)}, u32[]{:S(2)}, u32[]{:S(2)}) collective-permute-start(bf16[12,256,256]{2,1,0:T(8,128)(2,1)S(1)} %bitcast.26), channel_id=1, source_target_pairs={{0,28},{4,0},{8,4},{12,8},{16,12},{20,16},{24,20},{28,24},{1,29},{... | collective-permute-start | bytes 4718600 | tf_op jit(solution)/shard_map/ppermute | solution.py:20
  17.0 0.6 gather_fusion
  18.1 0.7 reshape.237.pick_ref
  19.1 0.6 dynamic-slice.4
  20.4 0.6 dynamic-slice.5
  21.0 0.7 gather_fusion.2
  21.8 0.6 broadcast_subtract_fusion
  22.7 1.2 copy.98.pts_ref
  25.3 114.8 %all_gather.20 = bf16[32,4,256]{2,1,0:T(4,128)(2,1)S(1)} all-gather(bf16[4,4,256]{2,1,0:T(4,128)(2,1)S(1)} %pad_maximum_fusion), channel_id=1, replica_groups=mesh['row'=8,'col'=4] {'row'}, dimensions={0}, use_global_device_ids=true | all-gather | bytes 73728 | tf_op jit(solution)/shard_map/all_gather | solution.py:175
  140.1 0.6 gather_fusion.1
  140.8 0.7 pad_convert_fusion.par_ref
  141.5 0.6 fusion.14.shift_ref
  142.2 40.4 %square_collocate.1 = (bf16[4,3,256,256]{3,2,1,0:T(8,128)(2,1)}, f32[4,6,1024]{2,1,0:T(8,128)}) custom-call(s32[4,36]{1,0:T(4,128)} %reshape.237.pick_ref, s32[4,6]{1,0:T(4,128)} %tiles_ref.3, s32[4,24]{1,0:T(4,128)} %fusion.14.shift_ref, bf16[4,4,3,256,256]{4,3,2,1,0:T(8,128)(2,1)} %bitcast.32, f32[4,4,8,256]{3,2,1,0:T(8,128)} %pad_convert_fusion.par_ref, ...), custom_call_target="tpu_custom_call" | custom-call | flops 25769803776 | bytes 20000000 | tf_op jit(solution)/shard_map/square_collocate/pallas_call | solution.py:200
  182.6 1.6 reshape.241
  184.2 18.0 %reduce-scatter.2.cloned.1.call-done = f32[24,256]{1,0:T(8,128)} async-done(((f32[24,1024]{1,0:T(8,128)}), f32[24,256]{1,0:T(8,128)}) %reduce-scatter.2.cloned.1.call-update) | async-done | bytes 24592 | tf_op jit(solution)/shard_map/reduce_scatter | solution.py:233
  202.1 0.9 fusion.5
  203.0 30.6 %all_gather.21 = f32[128,256]{1,0:T(8,128)S(1)} all-gather(f32[16,256]{1,0:T(8,128)S(1)} %fusion.5), channel_id=1, replica_groups=mesh['row'=8,'col'=4] {'row'}, dimensions={0}, use_global_device_ids=true | all-gather | bytes 147456 | tf_op jit(solution)/shard_map/all_gather | solution.py:244
  233.6 0.8 fusion.4
  234.4 30.5 %all_gather.22 = f32[128,256]{1,0:T(8,128)S(1)} all-gather(f32[16,256]{1,0:T(8,128)S(1)} %get-tuple-element.33), channel_id=1, replica_groups=mesh['row'=8,'col'=4] {'row'}, dimensions={0}, use_global_device_ids=true | all-gather | bytes 147456 | tf_op jit(solution)/shard_map/all_gather | solution.py:259
  264.9 6.9 %all_gather.23.field_ref = f32[128,1024]{1,0:T(8,128)} all-gather(f32[128,256]{1,0:T(8,128)S(1)} %all_gather.22), channel_id=1, replica_groups=mesh['row'=8,'col'=4] {'col'}, dimensions={1}, use_global_device_ids=true | all-gather | bytes 655360 | tf_op jit(solution)/shard_map/all_gather | solution.py:260
  271.8 31.2 %ks_blocks.1 = f32[4,3,256,256]{3,2,1,0:T(8,128)} custom-call(s32[4,6]{1,0:T(4,128)} %tiles_ref.3, s32[4,24]{1,0:T(4,128)} %fusion.14.shift_ref, s32[4,6]{1,0:T(4,128)} %get-tuple-element.30.holder_ref, f32[4,4,8,256]{3,2,1,0:T(8,128)} %pad_convert_fusion.par_ref, bf16[64,3,1024]{2,1,0:T(4,128)(2,1)} %copy.98.pts_ref, f32[128,1024]{1,0:T(8,128)} %all_gather.23.field_ref), custom_call_target="tpu_custom_call" | custom-call | flops 25769803776 | bytes 5000000 | tf_op jit(solution)/shard_map/ks_blocks/pallas_call | solution.py:264
  (74 shorter events, 3.6 us)
Async XLA Ops:
  7.2 1.4 copy-start
  7.2 9.5 %copy-start.3 = (s32[32,12]{0,1:T(8,128)S(1)}, s32[32,12]{0,1:T(8,128)}, u32[]{:S(2)}) copy-start(s32[32,12]{0,1:T(8,128)} %param.10) | copy-start | bytes 4612
  7.2 11.9 %copy-start.8 = (s32[8]{0:T(128)S(1)}, s32[8]{0:T(128)}, u32[]{:S(2)}) copy-start(s32[8]{0:T(128)} %param.14) | copy-start | bytes 100
  7.2 12.6 %copy-start.2 = (s32[4,6]{1,0:T(4,128)S(1)}, s32[4,6]{1,0:T(4,128)}, u32[]{:S(2)}) copy-start(s32[4,6]{1,0:T(4,128)} %tiles_ref.3) | copy-start | bytes 292
  7.2 134.9 %all-gather.3.cloned.1.call-start = ((), (), s32[]{:S(2)}) async-start(), calls=%async_computation.2 | async-start | bytes 7864320 | tf_op jit(solution)/shard_map/all_gather | solution.py:173
  7.9 14.6 %copy-start.6 = (bf16[4,3,256]{2,0,1:T(4,128)(2,1)S(1)}, bf16[4,3,256]{2,0,1:T(4,128)(2,1)}, u32[]{:S(2)}) copy-start(bf16[4,3,256]{2,0,1:T(4,128)(2,1)} %param.11) | copy-start | bytes 18436
  8.0 14.6 %copy-start.7 = (bf16[4,256]{1,0:T(4,128)(2,1)S(1)}, bf16[4,256]{1,0:T(4,128)(2,1)}, u32[]{:S(2)}) copy-start(bf16[4,256]{1,0:T(4,128)(2,1)} %param.12) | copy-start | bytes 6148
  8.0 14.7 %copy-start.1 = (bf16[64,3,1024]{2,0,1:T(8,128)(2,1)S(1)}, bf16[64,3,1024]{2,0,1:T(8,128)(2,1)}, u32[]{:S(2)}) copy-start(bf16[64,3,1024]{2,0,1:T(8,128)(2,1)} %param.15) | copy-start | bytes 1179652
  8.0 194.2 %reduce-scatter.2.cloned.1.call-start = ((), (), s32[]{:S(2)}) async-start(), calls=%async_computation.1 | async-start | bytes 122880 | tf_op jit(solution)/shard_map/reduce_scatter | solution.py:233
  8.6 133.5 %collective-permute-start = (bf16[12,256,256]{2,1,0:T(8,128)(2,1)S(1)}, bf16[12,256,256]{2,1,0:T(8,128)(2,1)}, u32[]{:S(2)}, u32[]{:S(2)}) collective-permute-start(bf16[12,256,256]{2,1,0:T(8,128)(2,1)S(1)} %bitcast.24), channel_id=1, source_target_pairs={{0,8},{4,12},{8,16},{12,20},{16,24},{20,28},{24,0},{28,4},{1,9},{5... | collective-permute-start | bytes 4718600 | tf_op jit(solution)/shard_map/ppermute | solution.py:20
  11.6 130.5 %collective-permute-start.1 = (bf16[12,256,256]{2,1,0:T(8,128)(2,1)S(1)}, bf16[12,256,256]{2,1,0:T(8,128)(2,1)}, u32[]{:S(2)}, u32[]{:S(2)}) collective-permute-start(bf16[12,256,256]{2,1,0:T(8,128)(2,1)S(1)} %bitcast.25), channel_id=1, source_target_pairs={{0,4},{4,8},{8,12},{12,16},{16,20},{20,24},{24,28},{28,0},{1,5},{5... | collective-permute-start | bytes 4718600 | tf_op jit(solution)/shard_map/ppermute | solution.py:20
  13.2 129.0 %collective-permute-start.2 = (bf16[12,256,256]{2,1,0:T(8,128)(2,1)S(1)}, bf16[12,256,256]{2,1,0:T(8,128)(2,1)}, u32[]{:S(2)}, u32[]{:S(2)}) collective-permute-start(bf16[12,256,256]{2,1,0:T(8,128)(2,1)S(1)} %bitcast.26), channel_id=1, source_target_pairs={{0,28},{4,0},{8,4},{12,8},{16,12},{20,16},{24,20},{28,24},{1,29},{... | collective-permute-start | bytes 4718600 | tf_op jit(solution)/shard_map/ppermute | solution.py:20
  16.4 125.8 %collective-permute-start.3 = (bf16[12,256,256]{2,1,0:T(8,128)(2,1)S(1)}, bf16[12,256,256]{2,1,0:T(8,128)(2,1)}, u32[]{:S(2)}, u32[]{:S(2)}) collective-permute-start(bf16[12,256,256]{2,1,0:T(8,128)(2,1)S(1)} %bitcast.27), channel_id=1, source_target_pairs={{0,24},{4,28},{8,0},{12,4},{16,8},{20,12},{24,16},{28,20},{1,25},{... | collective-permute-start | bytes 4718600 | tf_op jit(solution)/shard_map/ppermute | solution.py:20
  142.2 91.4 %copy-start.4 = (f32[16,256]{1,0:T(8,128)S(1)}, f32[16,256]{1,0:T(8,128)}, u32[]{:S(2)}) copy-start(f32[16,256]{1,0:T(8,128)} %param.17) | copy-start | bytes 49156
  142.2 91.4 %copy-start.5 = (f32[16,256]{1,0:T(8,128)S(1)}, f32[16,256]{1,0:T(8,128)}, u32[]{:S(2)}) copy-start(f32[16,256]{1,0:T(8,128)} %param.16) | copy-start | bytes 49156
Sparse Core Ops, SparseCore 0:
  9.6 49.0 all-gather.2
  184.3 17.8 reduce-scatter.1
